TPU v7x, 256 devices: a whole 4x4x8 slice. The times are simulated.
256 devices in a mesh: expert: 8 (over y, core), shard: 32 (over z, x).
Axes of the slice: x: 4, y: 4, z: 8, core: 2. Of those that a mesh axis runs over, the one named last changes fastest.
Arguments:
- master_down: float32 [16, 6400, 4096], P('expert', None, 'shard'), may hold values from -0.15625 to 0.15625
- second_down: bfloat16 [16, 6400, 4096], P('expert', None, 'shard'), may hold values from -0.0390625 to 0.0390625
- router_weight: float32 [4096, 16], P('shard', 'expert'), may hold values from -0.09375 to 0.09375
- router_gain: float32 [4096], P('shard'), may hold values from 0.25 to 1.75
Outputs:
- final_down: bfloat16 [16, 6400, 4096], P('expert', 'shard')
- scale_down: float32 [16, 6400], P('expert', 'shard')
- serve_router: bfloat16 [4096, 16], replicated
All inputs are finite; a program needn't handle non-finite values.
Results may differ from a plain program's by a relative error of at most 0.0085.
Values may be sent and summed in bfloat16 or wider, within the bound.
No kernel may reach another device: no remote copies, remote signals or barrier semaphores. Data moves between devices by JAX's collectives and lax.ppermute only.
A program may use at most 64 MiB of HBM per device.

v0:
```python
import jax
import jax.numpy as jnp
from jax import lax
from jax.sharding import PartitionSpec as P


def sent_to_all(x, axis):
    count = lax.axis_size(axis)
    return lax.all_to_all(jnp.broadcast_to(x[None], (count, *x.shape)), axis, 0, 0, tiled=True)


def taken_together(x, axis):
    everything = sent_to_all(x, axis)
    return jnp.sum(everything.astype(jnp.float32), axis=0)


def laid_out(parts, dim):
    dims = list(parts.shape[1:])
    dims[dim] *= parts.shape[0]
    return jnp.moveaxis(parts, 0, dim).reshape(dims)


def gathered_copies(x, axis, dim):
    parts = sent_to_all(x, axis)
    return laid_out(parts, dim)


def body(master_down, second_down, router_weight, router_gain):
    merged_down = master_down + second_down.astype(jnp.float32)
    total_down = taken_together(
        jnp.sum(merged_down * merged_down, axis=2).astype(jnp.bfloat16), "shard"
    ).astype(jnp.float32)
    scale_down = jnp.sqrt(total_down)
    narrow_down = (merged_down / jnp.expand_dims(scale_down, 2)).astype(jnp.bfloat16)
    final_down = lax.all_to_all(narrow_down, "shard", split_axis=1, concat_axis=2, tiled=True)
    scale_down = lax.dynamic_slice_in_dim(
        scale_down, lax.axis_index("shard") * final_down.shape[1], final_down.shape[1], axis=1
    )
    part_router = (router_weight * router_gain[:, None]).astype(jnp.bfloat16)
    row_router = gathered_copies(part_router, "shard", 0)
    serve_router = gathered_copies(row_router, "expert", 1)
    return (final_down, scale_down, serve_router)


def solution(mesh):
    placed = (
        P("expert", None, "shard"),
        P("expert", None, "shard"),
        P("shard", "expert"),
        P("shard"),
    )
    return jax.shard_map(
        body,
        mesh=mesh,
        in_specs=placed,
        out_specs=(P("expert", "shard", None), P("expert", "shard"), P()),
        check_vma=False,
    )
```

profile of v0, /device:TPU:6, one launch (start us, length us, event | category | flops | bytes accessed | tf_op | source)
XLA Modules:
  0.0 182.5 jit_solution(7028451042214102554)
XLA Ops:
  0.6 0.7 multiply_convert_fusion
  1.3 0.6 broadcast_in_dim.9
  1.9 11.6 %all-to-all-start.2 = ((bf16[32,128,2]{1,2,0:T(2,128)(2,1)}), bf16[32,128,2]{1,2,0:T(2,128)(2,1)S(1)}, u32[]{:S(2)}, u32[]{:S(2)}) async-start(bf16[32,128,2]{1,2,0:T(2,128)(2,1)} %broadcast_in_dim.9), calls=%async_computation.2 | async-start | bytes 32768 | tf_op jit(solution)/shard_map/all_to_all | solution.py:9
  13.5 0.0 copy-start
  13.5 5.7 %multiply_reduce_fusion = bf16[2,6400]{1,0:T(2,128)(2,1)S(1)} fusion(f32[2,6400,128]{2,1,0:T(8,128)} %param.4, bf16[2,6400,128]{2,1,0:T(8,128)(2,1)} %param.5), kind=kLoop, calls=%fused_computation.1 | loop fusion | flops 6540800 | bytes 9856000 | tf_op jit(solution)/shard_map/reduce_sum | solution.py:31
  19.3 2.1 %all-to-all-done.2 = bf16[32,128,2]{1,2,0:T(2,128)(2,1)S(1)} async-done(((bf16[32,128,2]{1,2,0:T(2,128)(2,1)}), bf16[32,128,2]{1,2,0:T(2,128)(2,1)S(1)}, u32[]{:S(2)}, u32[]{:S(2)}) %all-to-all-start.2) | async-done | bytes 16416 | tf_op jit(solution)/shard_map/all_to_all | solution.py:9
  21.4 0.4 broadcast_in_dim.8
  21.8 30.1 %all_to_all.33 = bf16[32,2,6400]{2,1,0:T(2,128)(2,1)} all-to-all(bf16[32,2,6400]{2,1,0:T(2,128)(2,1)S(1)} %broadcast_in_dim.8), channel_id=1, replica_groups=mesh['expert'=8,'shard'=32] {'shard'}, dimensions={0} | all-to-all | bytes 1638400 | tf_op jit(solution)/shard_map/all_to_all | solution.py:9
  52.0 0.7 broadcast_in_dim.11
  52.7 4.5 %all-to-all-start.3 = ((bf16[8,4096,2]{1,2,0:T(2,128)(2,1)}), bf16[8,4096,2]{1,2,0:T(2,128)(2,1)S(1)}, u32[]{:S(2)}, u32[]{:S(2)}) async-start(bf16[8,4096,2]{1,2,0:T(2,128)(2,1)} %broadcast_in_dim.11), calls=%async_computation.3 | async-start | bytes 262144 | tf_op jit(solution)/shard_map/all_to_all | solution.py:9
  57.2 1.3 convert_reduce_fusion
  58.5 0.1 sqrt.7
  58.6 0.0 copy-done
  58.6 4.7 %divide_convert_fusion = bf16[2,6400,128]{2,1,0:T(8,128)(2,1)S(1)} fusion(f32[2,6400,128]{2,1,0:T(8,128)} %param.4, bf16[2,6400,128]{2,1,0:T(8,128)(2,1)S(1)} %copy-done, f32[2,6400]{1,0:T(2,128)S(1)} %sqrt.7), kind=kLoop, calls=%fused_computation | loop fusion | flops 6553600 | bytes 13158400 | tf_op jit(solution)/shard_map/convert_element_type | solution.py:34
  63.3 27.9 %copy.31 = bf16[2,6400,128]{2,0,1:T(2,128)(2,1)} copy(bf16[2,6400,128]{2,1,0:T(8,128)(2,1)S(1)} %divide_convert_fusion) | data formatting | bytes 6553600 | tf_op jit(solution)/shard_map/convert_element_type | solution.py:34
  91.2 0.0 all-to-all-done.3
  91.2 5.6 %all-to-all-start.1 = ((bf16[2,6400,128]{2,0,1:T(2,128)(2,1)}), bf16[2,6400,128]{2,0,1:T(2,128)(2,1)S(1)}, u32[]{:S(2)}, u32[]{:S(2)}) async-start(bf16[2,6400,128]{2,0,1:T(2,128)(2,1)} %copy.31), calls=%async_computation.1 | async-start | bytes 6553600 | tf_op jit(solution)/shard_map/all_to_all | solution.py:35
  96.8 0.7 reshape.18
  97.5 0.7 constant_dynamic-slice_fusion
  98.1 75.6 %all-to-all-done.1 = bf16[2,6400,128]{2,0,1:T(2,128)(2,1)S(1)} async-done(((bf16[2,6400,128]{2,0,1:T(2,128)(2,1)}), bf16[2,6400,128]{2,0,1:T(2,128)(2,1)S(1)}, u32[]{:S(2)}, u32[]{:S(2)}) %all-to-all-start.1) | async-done | bytes 3276832 | tf_op jit(solution)/shard_map/all_to_all | solution.py:35
  173.8 2.5 %copy.32 = bf16[2,200,32,128]{3,2,1,0:T(8,128)(2,1)} copy(bf16[2,200,32,128]{3,0,1,2:T(2,128)(2,1)S(1)} %bitcast.9) | data formatting | bytes 6553600 | tf_op jit(solution)/shard_map/all_to_all | solution.py:35
  176.3 6.2 %all_to_all.26 = bf16[2,200,4096]{2,1,0:T(8,128)(2,1)} reshape(bf16[2,200,32,128]{3,2,1,0:T(8,128)(2,1)} %copy.32) | data formatting | bytes 6553600 | tf_op jit(solution)/shard_map/all_to_all | solution.py:35
Async XLA Ops:
  1.9 19.5 %all-to-all-start.2 = ((bf16[32,128,2]{1,2,0:T(2,128)(2,1)}), bf16[32,128,2]{1,2,0:T(2,128)(2,1)S(1)}, u32[]{:S(2)}, u32[]{:S(2)}) async-start(bf16[32,128,2]{1,2,0:T(2,128)(2,1)} %broadcast_in_dim.9), calls=%async_computation.2 | async-start | bytes 32768 | tf_op jit(solution)/shard_map/all_to_all | solution.py:9
  13.5 45.1 %copy-start = (bf16[2,6400,128]{2,1,0:T(8,128)(2,1)S(1)}, bf16[2,6400,128]{2,1,0:T(8,128)(2,1)}, u32[]{:S(2)}) copy-start(bf16[2,6400,128]{2,1,0:T(8,128)(2,1)} %param.5) | copy-start | bytes 9830404
  52.7 38.5 %all-to-all-start.3 = ((bf16[8,4096,2]{1,2,0:T(2,128)(2,1)}), bf16[8,4096,2]{1,2,0:T(2,128)(2,1)S(1)}, u32[]{:S(2)}, u32[]{:S(2)}) async-start(bf16[8,4096,2]{1,2,0:T(2,128)(2,1)} %broadcast_in_dim.11), calls=%async_computation.3 | async-start | bytes 262144 | tf_op jit(solution)/shard_map/all_to_all | solution.py:9
  91.2 82.6 %all-to-all-start.1 = ((bf16[2,6400,128]{2,0,1:T(2,128)(2,1)}), bf16[2,6400,128]{2,0,1:T(2,128)(2,1)S(1)}, u32[]{:S(2)}, u32[]{:S(2)}) async-start(bf16[2,6400,128]{2,0,1:T(2,128)(2,1)} %copy.31), calls=%async_computation.1 | async-start | bytes 6553600 | tf_op jit(solution)/shard_map/all_to_all | solution.py:35
where the time goes:
time: 184 us; the launch traced here: 183 us
  waiting for transfers between devices  77.8 us (42%)
  local copies, waits for them, and re-layouts  39.8 us (22%)
  blocking collectives  30.1 us (16%)
  starting transfers between devices  21.6 us (12%)
  other arithmetic  12.5 us (7%)
    all_to_all x1, waiting for transfers between devices, body(): lax.all_to_all(narrow_down, 'shard', split_axis=1, concat_axis=2, tiled=T...  75.6 us
    all_to_all x1, blocking collectives, sent_to_all(): lax.all_to_all(jnp.broadcast_to(x[None], (count, *x.shape)), axis, 0, 0,...  30.1 us
    convert_element_type x1, local copies, waits for them, and re-layouts, body(): (merged_down / jnp.expand_dims(scale_down, 2)).astype(jnp.bfloat16)  27.9 us
    all_to_all x2, starting transfers between devices, sent_to_all(): lax.all_to_all(jnp.broadcast_to(x[None], (count, *x.shape)), axis, 0, 0,...  16 us
    all_to_all x2, local copies, waits for them, and re-layouts, body(): lax.all_to_all(narrow_down, 'shard', split_axis=1, concat_axis=2, tiled=T...  8.72 us
    reduce_sum x1, other arithmetic, body(): jnp.sum(merged_down * merged_down, axis=2).astype(jnp.bfloat16)  5.75 us
    all_to_all x1, starting transfers between devices, body(): lax.all_to_all(narrow_down, 'shard', split_axis=1, concat_axis=2, tiled=T...  5.57 us
    convert_element_type x1, other arithmetic, body(): (merged_down / jnp.expand_dims(scale_down, 2)).astype(jnp.bfloat16)  4.74 us
  transfers between devices with their start and end apart: 3, of which 2 were waited for; matrix products, arithmetic and copies ran while one was open for 23% of the time, Pallas kernels for 0%

commit v1 on v0

v1 whole, which is shorter than its diff:
```python
import jax
import jax.numpy as jnp
from jax import lax
from jax.experimental import pallas as pl
from jax.experimental.pallas import tpu as pltpu
from jax.sharding import PartitionSpec as P


def packed_kernel(master_ref, second_ref, out_ref):
    out_ref[...] = (master_ref[...] + second_ref[...].astype(jnp.float32)).astype(jnp.bfloat16)


def packed(master, second, expert, group):
    _, shards, rows, lanes = master.shape
    taken = pl.BlockSpec((None, group, rows, lanes), lambda s: (expert, s, 0, 0))
    return pl.pallas_call(
        packed_kernel,
        grid=(shards // group,),
        in_specs=[taken, taken],
        out_specs=pl.BlockSpec((group, rows, lanes), lambda s: (s, 0, 0)),
        out_shape=jax.ShapeDtypeStruct((shards, rows, lanes), jnp.bfloat16),
        name="packed",
    )(master, second)


def normed_kernel(parts_ref, *refs):
    out_ref, scale_ref = refs[-2:]
    shards, rows, lanes = parts_ref.shape
    total = jnp.zeros((rows, lanes), jnp.float32)
    for s in range(shards):
        part = parts_ref[s].astype(jnp.float32)
        total = total + part * part
    scale = jnp.sqrt(jnp.sum(total, axis=1, keepdims=True))
    scale_ref[...] = jnp.broadcast_to(scale, scale_ref.shape)
    inverse = jnp.broadcast_to(1.0 / scale, (rows, lanes))
    for s in range(shards):
        part = parts_ref[s].astype(jnp.float32)
        out_ref[:, s * lanes:(s + 1) * lanes] = (part * inverse).astype(jnp.bfloat16)


def normed(parts, expert, experts, block, before):
    shards, rows, lanes = parts.shape
    width = shards * lanes
    return pl.pallas_call(
        normed_kernel,
        grid=(rows // block,),
        in_specs=[pl.BlockSpec((shards, block, lanes), lambda r: (0, r, 0))]
        + [pl.BlockSpec(memory_space=pl.ANY) for _ in before],
        out_specs=[
            pl.BlockSpec((None, block, width), lambda r: (expert, r, 0)),
            pl.BlockSpec((block, lanes), lambda r: (r, 0)),
        ],
        out_shape=[
            jax.ShapeDtypeStruct((experts, rows, width), jnp.bfloat16),
            jax.ShapeDtypeStruct((rows, lanes), jnp.float32),
        ],
        input_output_aliases={1: 0} if before else {},
        name="normed",
    )(parts, *before)


def sent_to_all(x, axis):
    count = lax.axis_size(axis)
    return lax.all_to_all(jnp.broadcast_to(x[None], (count, *x.shape)), axis, 0, 0, tiled=True)


def laid_out(parts, dim):
    dims = list(parts.shape[1:])
    dims[dim] *= parts.shape[0]
    return jnp.moveaxis(parts, 0, dim).reshape(dims)


def gathered_copies(x, axis, dim):
    return laid_out(sent_to_all(x, axis), dim)


def body(master_down, second_down, router_weight, router_gain):
    shards = lax.axis_size("shard")
    experts, rows, lanes = master_down.shape
    cut = (experts, shards, rows // shards, lanes)
    master, second = master_down.reshape(cut), second_down.reshape(cut)
    final, scales = (), []
    received = []
    for expert in range(experts):
        sent = packed(master, second, expert, 8)
        received.append(lax.all_to_all(sent, "shard", 0, 0, tiled=True))
    for expert in range(experts):
        out, scale = normed(received[expert], expert, experts, 40, final)
        final = (out,)
        scales.append(scale[:, 0])
    scale_down = jnp.stack(scales)
    part_router = (router_weight * router_gain[:, None]).astype(jnp.bfloat16)
    row_router = gathered_copies(part_router, "shard", 0)
    serve_router = gathered_copies(row_router, "expert", 1)
    return (final[0], scale_down, serve_router)


def solution(mesh):
    placed = (
        P("expert", None, "shard"),
        P("expert", None, "shard"),
        P("shard", "expert"),
        P("shard"),
    )
    return jax.shard_map(
        body,
        mesh=mesh,
        in_specs=placed,
        out_specs=(P("expert", "shard", None), P("expert", "shard"), P()),
        check_vma=False,
    )
```

time: 184 us -> 132 us (0.72)
  local copies, waits for them, and re-layouts: 39.8 us -> 3.72 us
  Pallas kernels: 0 us -> 17.6 us
  other arithmetic: 12.5 us -> 1.28 us
  blocking collectives: 30.1 us -> 19.3 us
  starting transfers between devices: 21.6 us -> 15.7 us
  waiting for transfers between devices: 77.8 us -> 72.7 us
    convert_element_type x1 -> x0, local copies, waits for them, and re-layouts: 27.9 us -> none  [body(): (merged_down / jnp.expand_dims(scale_down, 2)).astype(jnp.bfloat16)]
    pallas_call x0 -> x4, Pallas kernels: none -> 17.6 us  [the longest x2 9.12 us: normed(): pl.pallas_call(normed_kernel, grid=(rows // block,), in_specs=[pl.BlockSp...]
    all_to_all x2 -> x1, starting transfers between devices: 16 us -> 4.47 us  [sent_to_all(): lax.all_to_all(jnp.broadcast_to(x[None], (count, *x.shape)), axis, 0, 0,...]
    all_to_all x1, blocking collectives: 30.1 us -> 19.3 us  [sent_to_all(): lax.all_to_all(jnp.broadcast_to(x[None], (count, *x.shape)), axis, 0, 0,...]
    all_to_all x2 -> x0, local copies, waits for them, and re-layouts: 8.72 us -> none  [body(): lax.all_to_all(narrow_down, 'shard', split_axis=1, concat_axis=2, tiled=T...]
    reduce_sum x2 -> x0, other arithmetic: 7.08 us -> none  [the longest x1 5.75 us: body(): jnp.sum(merged_down * merged_down, axis=2).astype(jnp.bfloat16)]
    all_to_all x1 -> x2, starting transfers between devices: 5.57 us -> 11.2 us  [body(): received.append(lax.all_to_all(sent, 'shard', 0, 0, tiled=True))]
    all_to_all x1 -> x2, waiting for transfers between devices: 75.6 us -> 70.8 us  [body(): received.append(lax.all_to_all(sent, 'shard', 0, 0, tiled=True))]
  transfers between devices with their start and end apart: 3 -> 3, of which waited for: 2 -> 3; matrix products, arithmetic and copies ran while one was open for 23% -> 1% of each run, Pallas kernels for 0% -> 10%
where the time goes in v1:
time: 132 us; the launch traced here: 131 us
  waiting for transfers between devices  72.7 us (55%)
  blocking collectives  19.3 us (15%)
  Pallas kernels  17.6 us (13%)
  starting transfers between devices  15.7 us (12%)
  local copies, waits for them, and re-layouts  3.72 us (3%)
    all_to_all x2, waiting for transfers between devices, body(): received.append(lax.all_to_all(sent, 'shard', 0, 0, tiled=True))  70.8 us
    all_to_all x1, blocking collectives, sent_to_all(): lax.all_to_all(jnp.broadcast_to(x[None], (count, *x.shape)), axis, 0, 0,...  19.3 us
    all_to_all x2, starting transfers between devices, body(): received.append(lax.all_to_all(sent, 'shard', 0, 0, tiled=True))  11.2 us
    pallas_call x2, Pallas kernels, normed(): pl.pallas_call(normed_kernel, grid=(rows // block,), in_specs=[pl.BlockSp...  9.12 us
    pallas_call x2, Pallas kernels, packed(): pl.pallas_call(packed_kernel, grid=(shards // group,), in_specs=[taken, t...  8.5 us
    all_to_all x1, starting transfers between devices, sent_to_all(): lax.all_to_all(jnp.broadcast_to(x[None], (count, *x.shape)), axis, 0, 0,...  4.47 us
  transfers between devices with their start and end apart: 3, of which 3 were waited for; matrix products, arithmetic and copies ran while one was open for 1% of the time, Pallas kernels for 10%

profile of v1, /device:TPU:6, one launch (start us, length us, event | category | flops | bytes accessed | tf_op | source)
XLA Modules:
  0.0 131.0 jit_solution(6359667905585547721)
XLA Ops:
  0.6 0.7 multiply_convert_fusion
  1.3 19.3 %all_to_all.20 = bf16[32,128,2]{1,2,0:T(2,128)(2,1)S(1)} all-to-all(bf16[32,128,2]{1,2,0:T(2,128)(2,1)S(1)} %broadcast_in_dim.6), channel_id=1, replica_groups=mesh['expert'=8,'shard'=32] {'shard'}, dimensions={0} | all-to-all | bytes 32768 | tf_op jit(solution)/shard_map/all_to_all | solution.py:64
  20.7 0.7 broadcast_in_dim.16
  21.4 4.5 %all-to-all-start.3 = ((bf16[8,4096,2]{1,2,0:T(2,128)(2,1)}), bf16[8,4096,2]{1,2,0:T(2,128)(2,1)S(1)}, u32[]{:S(2)}, u32[]{:S(2)}) async-start(bf16[8,4096,2]{1,2,0:T(2,128)(2,1)} %broadcast_in_dim.16), calls=%async_computation.3 | async-start | bytes 262144 | tf_op jit(solution)/shard_map/all_to_all | solution.py:64
  25.9 4.2 %packed.3 = bf16[32,200,128]{2,1,0:T(8,128)(2,1)} custom-call(f32[2,32,200,128]{3,2,1,0:T(8,128)} %bitcast.8, bf16[2,32,200,128]{3,2,1,0:T(8,128)(2,1)} %bitcast.10), custom_call_target="tpu_custom_call" | custom-call | tf_op jit(solution)/shard_map/packed/pallas_call | solution.py:16
  30.1 1.9 %all-to-all-done.3 = bf16[8,4096,2]{1,2,0:T(2,128)(2,1)S(1)} async-done(((bf16[8,4096,2]{1,2,0:T(2,128)(2,1)}), bf16[8,4096,2]{1,2,0:T(2,128)(2,1)S(1)}, u32[]{:S(2)}, u32[]{:S(2)}) %all-to-all-start.3) | async-done | bytes 131104 | tf_op jit(solution)/shard_map/all_to_all | solution.py:64
  32.0 5.7 %all-to-all-start.1 = ((bf16[32,200,128]{2,1,0:T(8,128)(2,1)}), bf16[32,200,128]{2,1,0:T(8,128)(2,1)S(1)}, u32[]{:S(2)}, u32[]{:S(2)}) async-start(bf16[32,200,128]{2,1,0:T(8,128)(2,1)} %packed.3), calls=%async_computation.1 | async-start | bytes 3276800 | tf_op jit(solution)/shard_map/all_to_all | solution.py:86
  37.6 4.3 %packed.2 = bf16[32,200,128]{2,1,0:T(8,128)(2,1)} custom-call(f32[2,32,200,128]{3,2,1,0:T(8,128)} %bitcast.9, bf16[2,32,200,128]{3,2,1,0:T(8,128)(2,1)} %bitcast.11), custom_call_target="tpu_custom_call" | custom-call | tf_op jit(solution)/shard_map/packed/pallas_call | solution.py:16
  41.9 36.6 %all-to-all-done.1.parts_ref = bf16[32,200,128]{2,1,0:T(8,128)(2,1)S(1)} async-done(((bf16[32,200,128]{2,1,0:T(8,128)(2,1)}), bf16[32,200,128]{2,1,0:T(8,128)(2,1)S(1)}, u32[]{:S(2)}, u32[]{:S(2)}) %all-to-all-start.1) | async-done | bytes 1638432 | tf_op jit(solution)/shard_map/all_to_all | solution.py:86
  78.5 0.0 copy-start
  78.5 5.6 %all-to-all-start = ((bf16[32,200,128]{2,1,0:T(8,128)(2,1)}), bf16[32,200,128]{2,1,0:T(8,128)(2,1)S(1)}, u32[]{:S(2)}, u32[]{:S(2)}) async-start(bf16[32,200,128]{2,1,0:T(8,128)(2,1)} %packed.2), calls=%async_computation | async-start | bytes 3276800 | tf_op jit(solution)/shard_map/all_to_all | solution.py:86
  84.1 0.7 reshape.20
  84.8 0.0 copy-done
  84.8 4.6 %normed.2 = (bf16[2,200,4096]{2,1,0:T(8,128)(2,1)}, f32[200,128]{1,0:T(8,128)}) custom-call(bf16[32,200,128]{2,1,0:T(8,128)(2,1)} %copy-done), custom_call_target="tpu_custom_call" | custom-call | tf_op jit(solution)/shard_map/normed/pallas_call | solution.py:44
  89.4 0.0 copy-start.2
  89.4 34.2 %all-to-all-done.parts_ref = bf16[32,200,128]{2,1,0:T(8,128)(2,1)S(1)} async-done(((bf16[32,200,128]{2,1,0:T(8,128)(2,1)}), bf16[32,200,128]{2,1,0:T(8,128)(2,1)S(1)}, u32[]{:S(2)}, u32[]{:S(2)}) %all-to-all-start) | async-done | bytes 1638432 | tf_op jit(solution)/shard_map/all_to_all | solution.py:86
  123.5 0.0 copy-start.1
  123.5 1.2 copy-done.1
  124.7 4.6 %normed.3 = (bf16[2,200,4096]{2,1,0:T(8,128)(2,1)}, f32[200,128]{1,0:T(8,128)}) custom-call(bf16[32,200,128]{2,1,0:T(8,128)(2,1)} %copy-done.1, bf16[2,200,4096]{2,1,0:T(8,128)(2,1)} %get-tuple-element.7.refs_0_), custom_call_target="tpu_custom_call", output_to_operand_aliasing={{0}: (1, {})} | custom-call | tf_op jit(solution)/shard_map/normed/pallas_call | solution.py:44
  129.3 1.0 slice_reduce_fusion
  130.3 0.0 copy-done.2
  130.3 0.1 slice_reduce_fusion.1
  130.4 0.6 pad_maximum_fusion
  (1 shorter events, 0.0 us)
Async XLA Ops:
  21.4 10.6 %all-to-all-start.3 = ((bf16[8,4096,2]{1,2,0:T(2,128)(2,1)}), bf16[8,4096,2]{1,2,0:T(2,128)(2,1)S(1)}, u32[]{:S(2)}, u32[]{:S(2)}) async-start(bf16[8,4096,2]{1,2,0:T(2,128)(2,1)} %broadcast_in_dim.16), calls=%async_computation.3 | async-start | bytes 262144 | tf_op jit(solution)/shard_map/all_to_all | solution.py:64
  32.0 46.5 %all-to-all-start.1 = ((bf16[32,200,128]{2,1,0:T(8,128)(2,1)}), bf16[32,200,128]{2,1,0:T(8,128)(2,1)S(1)}, u32[]{:S(2)}, u32[]{:S(2)}) async-start(bf16[32,200,128]{2,1,0:T(8,128)(2,1)} %packed.3), calls=%async_computation.1 | async-start | bytes 3276800 | tf_op jit(solution)/shard_map/all_to_all | solution.py:86
  78.5 6.3 %copy-start = (bf16[32,200,128]{2,1,0:T(8,128)(2,1)}, bf16[32,200,128]{2,1,0:T(8,128)(2,1)S(1)}, u32[]{:S(2)}) copy-start(bf16[32,200,128]{2,1,0:T(8,128)(2,1)S(1)} %all-to-all-done.1.parts_ref) | copy-start | bytes 4915204
  78.5 45.0 %all-to-all-start = ((bf16[32,200,128]{2,1,0:T(8,128)(2,1)}), bf16[32,200,128]{2,1,0:T(8,128)(2,1)S(1)}, u32[]{:S(2)}, u32[]{:S(2)}) async-start(bf16[32,200,128]{2,1,0:T(8,128)(2,1)} %packed.2), calls=%async_computation | async-start | bytes 3276800 | tf_op jit(solution)/shard_map/all_to_all | solution.py:86
  89.4 40.9 %copy-start.2 = (f32[200,128]{1,0:T(8,128)S(1)}, f32[200,128]{1,0:T(8,128)}, u32[]{:S(2)}) copy-start(f32[200,128]{1,0:T(8,128)} %get-tuple-element.9) | copy-start | bytes 307204
  123.5 1.2 copy-start.1

commit v2 on v0

v2 whole, which is shorter than its diff:
```python
import jax
import jax.numpy as jnp
from jax import lax
from jax.experimental import pallas as pl
from jax.experimental.pallas import tpu as pltpu
from jax.sharding import PartitionSpec as P

PACK_GROUP = 4
NORM_ROWS = 40


def packed_kernel(master_ref, second_ref, out_ref, master_vmem, second_vmem, out_vmem, master_sem, second_sem, out_sem):
    steps = out_ref.shape[0] // PACK_GROUP

    def at(step):
        return pl.ds(step * PACK_GROUP, PACK_GROUP)

    def copies(step):
        return (
            pltpu.make_async_copy(master_ref.at[:, at(step)], master_vmem.at[:, at(step)], master_sem.at[step]),
            pltpu.make_async_copy(second_ref.at[:, at(step)], second_vmem.at[:, at(step)], second_sem.at[step]),
        )

    def copy_out(step):
        return pltpu.make_async_copy(out_vmem.at[at(step)], out_ref.at[at(step)], out_sem.at[step])

    for step in range(steps):
        for copy in copies(step):
            copy.start()
    for step in range(steps):
        for copy in copies(step):
            copy.wait()
        for s in range(step * PACK_GROUP, (step + 1) * PACK_GROUP):
            out_vmem[s] = (master_vmem[:, s] + second_vmem[:, s].astype(jnp.float32)).astype(jnp.bfloat16)
        copy_out(step).start()
    for step in range(steps):
        copy_out(step).wait()


def packed(master, second):
    experts, shards, rows, lanes = master.shape
    steps = shards // PACK_GROUP
    sent = jax.ShapeDtypeStruct((shards, experts, rows, lanes), jnp.bfloat16)
    return pl.pallas_call(
        packed_kernel,
        in_specs=[pl.BlockSpec(memory_space=pl.ANY)] * 2,
        out_specs=pl.BlockSpec(memory_space=pl.ANY),
        out_shape=sent,
        scratch_shapes=[
            pltpu.VMEM(master.shape, jnp.float32),
            pltpu.VMEM(second.shape, jnp.bfloat16),
            pltpu.VMEM(sent.shape, jnp.bfloat16),
            pltpu.SemaphoreType.DMA((steps,)),
            pltpu.SemaphoreType.DMA((steps,)),
            pltpu.SemaphoreType.DMA((steps,)),
        ],
        name="packed",
    )(master, second)


def normed_kernel(parts_ref, out_ref, scale_ref, out_vmem, total_vmem, sems):
    shards, experts, rows, lanes = parts_ref.shape
    blocks = rows // NORM_ROWS

    def copy(expert, block):
        at = (expert, pl.ds(block * NORM_ROWS, NORM_ROWS))
        return pltpu.make_async_copy(out_vmem.at[at], out_ref.at[at], sems.at[expert * blocks + block])

    for expert in range(experts):
        for block in range(blocks):
            at = pl.ds(block * NORM_ROWS, NORM_ROWS)
            total = jnp.zeros((NORM_ROWS, lanes), jnp.float32)
            for s in range(shards):
                part = parts_ref[s, expert, at].astype(jnp.float32)
                total = total + part * part
            total_vmem[expert, at] = total
            scale = jnp.sqrt(jnp.sum(total, axis=1, keepdims=True))
            inverse = jnp.broadcast_to(1.0 / scale, total.shape)
            for s in range(shards):
                part = parts_ref[s, expert, at].astype(jnp.float32)
                out_vmem[expert, at, pl.ds(s * lanes, lanes)] = (part * inverse).astype(jnp.bfloat16)
            copy(expert, block).start()
    for expert in range(experts):
        turned = jnp.transpose(total_vmem[expert])
        scale_ref[pl.ds(expert, 1)] = jnp.sqrt(jnp.sum(turned, axis=0, keepdims=True))
    for expert in range(experts):
        for block in range(blocks):
            copy(expert, block).wait()


def normed(parts):
    shards, experts, rows, lanes = parts.shape
    width = shards * lanes
    return pl.pallas_call(
        normed_kernel,
        in_specs=[pl.BlockSpec(memory_space=pltpu.VMEM)],
        out_specs=[pl.BlockSpec(memory_space=pl.ANY), pl.BlockSpec(memory_space=pltpu.VMEM)],
        out_shape=[
            jax.ShapeDtypeStruct((experts, rows, width), jnp.bfloat16),
            jax.ShapeDtypeStruct((experts, rows), jnp.float32),
        ],
        scratch_shapes=[
            pltpu.VMEM((experts, rows, width), jnp.bfloat16),
            pltpu.VMEM((experts, rows, lanes), jnp.float32),
            pltpu.SemaphoreType.DMA((experts * rows // NORM_ROWS,)),
        ],
        name="normed",
    )(pltpu.with_memory_space_constraint(parts, pltpu.VMEM))


def body(master_down, second_down, router_weight, router_gain):
    shards = lax.axis_size("shard")
    experts, rows, lanes = master_down.shape
    cut = (experts, shards, rows // shards, lanes)
    sent = packed(master_down.reshape(cut), second_down.reshape(cut))
    received = lax.all_to_all(sent, "shard", 0, 0, tiled=True)
    final_down, scale_down = normed(received)
    part_router = (router_weight * router_gain[:, None]).astype(jnp.bfloat16).T
    row_router = lax.all_gather(part_router, "shard", axis=1, tiled=True)
    serve_router = lax.all_gather(row_router, "expert", axis=0, tiled=True).T
    return (final_down, scale_down, serve_router)


def solution(mesh):
    placed = (
        P("expert", None, "shard"),
        P("expert", None, "shard"),
        P("shard", "expert"),
        P("shard"),
    )
    return jax.shard_map(
        body,
        mesh=mesh,
        in_specs=placed,
        out_specs=(P("expert", "shard", None), P("expert", "shard"), P()),
        check_vma=False,
    )
```

time: 184 us -> 140 us (0.76)
  blocking collectives: 30.1 us -> 116 us
  waiting for transfers between devices: 77.8 us -> 0.01 us
  local copies, waits for them, and re-layouts: 39.8 us -> 0.72 us
  other arithmetic: 12.5 us -> 0.01 us
  starting transfers between devices: 21.6 us -> 11.6 us
  Pallas kernels: 0 us -> 8.25 us
    all_gather x0 -> x2, blocking collectives: none -> 116 us  [the longest x1 103 us: body(): row_router = lax.all_gather(part_router, 'shard', axis=1, tiled=True)]
    all_to_all x3 -> x1, waiting for transfers between devices: 77.8 us -> 0.01 us  [body(): received = lax.all_to_all(sent, 'shard', 0, 0, tiled=True)]
    all_to_all x1 -> x0, blocking collectives: 30.1 us -> none  [sent_to_all(): lax.all_to_all(jnp.broadcast_to(x[None], (count, *x.shape)), axis, 0, 0,...]
    convert_element_type x1 -> x0, local copies, waits for them, and re-layouts: 27.9 us -> none  [body(): (merged_down / jnp.expand_dims(scale_down, 2)).astype(jnp.bfloat16)]
    all_to_all x3 -> x1, starting transfers between devices: 21.6 us -> 11.6 us  [body(): received = lax.all_to_all(sent, 'shard', 0, 0, tiled=True)]
    all_to_all x2 -> x0, local copies, waits for them, and re-layouts: 8.72 us -> none  [body(): lax.all_to_all(narrow_down, 'shard', split_axis=1, concat_axis=2, tiled=T...]
    pallas_call x0 -> x2, Pallas kernels: none -> 8.25 us  [the longest x1 5.55 us: packed(): pl.pallas_call(packed_kernel, in_specs=[pl.BlockSpec(memory_space=pl.ANY)...]
    reduce_sum x2 -> x0, other arithmetic: 7.08 us -> none  [the longest x1 5.75 us: body(): jnp.sum(merged_down * merged_down, axis=2).astype(jnp.bfloat16)]
  transfers between devices with their start and end apart: 3 -> 1, of which waited for: 2 -> 0; matrix products, arithmetic and copies ran while one was open for 23% -> 1% of each run, Pallas kernels for 0% -> 0%
where the time goes in v2:
time: 140 us; the launch traced here: 137 us
  blocking collectives  116 us (83%)
  starting transfers between devices  11.6 us (8%)
  Pallas kernels  8.25 us (6%)
    all_gather x1, blocking collectives, body(): row_router = lax.all_gather(part_router, 'shard', axis=1, tiled=True)  103 us
    all_gather x1, blocking collectives, body(): serve_router = lax.all_gather(row_router, 'expert', axis=0, tiled=True).T  13.3 us
    all_to_all x1, starting transfers between devices, body(): received = lax.all_to_all(sent, 'shard', 0, 0, tiled=True)  11.6 us
    pallas_call x1, Pallas kernels, packed(): pl.pallas_call(packed_kernel, in_specs=[pl.BlockSpec(memory_space=pl.ANY)...  5.55 us
  transfers between devices with their start and end apart: 1, of which 0 were waited for; matrix products, arithmetic and copies ran while one was open for 1% of the time, Pallas kernels for 0%

profile of v2, /device:TPU:6, one launch (start us, length us, event | category | flops | bytes accessed | tf_op | source)
XLA Modules:
  0.0 137.3 jit_solution(18338510968726401718)
XLA Ops:
  0.6 5.5 %packed.1 = bf16[32,2,200,128]{3,2,1,0:T(8,128)(2,1)} custom-call(f32[2,32,200,128]{3,2,1,0:T(8,128)} %bitcast.6, bf16[2,32,200,128]{3,2,1,0:T(8,128)(2,1)} %bitcast.7), custom_call_target="tpu_custom_call" | custom-call | tf_op jit(solution)/shard_map/packed/pallas_call | solution.py:44
  6.2 0.0 copy-start
  6.2 0.0 copy-start.1
  6.2 11.6 %all-to-all-start = ((bf16[32,2,200,128]{3,2,1,0:T(8,128)(2,1)}), bf16[32,2,200,128]{3,2,1,0:T(8,128)(2,1)S(1)}, u32[]{:S(2)}, u32[]{:S(2)}) async-start(bf16[32,2,200,128]{3,2,1,0:T(8,128)(2,1)} %packed.1), calls=%async_computation | async-start | bytes 6553600 | tf_op jit(solution)/shard_map/all_to_all | solution.py:116
  17.8 0.0 copy-done
  17.8 0.0 copy-done.1
  17.8 102.8 %all_gather.6 = bf16[2,4096]{1,0:T(2,128)(2,1)S(1)} all-gather(bf16[2,128]{1,0:T(2,128)(2,1)S(1)} %fusion), channel_id=1, replica_groups=mesh['expert'=8,'shard'=32] {'shard'}, dimensions={1}, use_global_device_ids=true | all-gather | bytes 16896 | tf_op jit(solution)/shard_map/all_gather | solution.py:119
  120.6 13.3 %all-gather = bf16[8,2,4096]{2,1,0:T(2,128)(2,1)S(1)} all-gather(bf16[1,2,4096]{2,1,0:T(2,128)(2,1)S(1)} %bitcast.9), channel_id=1, replica_groups=mesh['expert'=8,'shard'=32] {'expert'}, dimensions={0}, use_global_device_ids=true | all-gather | bytes 147456 | tf_op jit(solution)/shard_map/all_gather | solution.py:120
  133.9 0.7 reshape.16
  134.6 0.0 all-to-all-done.parts_ref
  134.6 2.7 %normed.1 = (bf16[2,200,4096]{2,1,0:T(8,128)(2,1)}, f32[2,200]{1,0:T(2,128)}) custom-call(bf16[32,2,200,128]{3,2,1,0:T(8,128)(2,1)S(1)} %all-to-all-done.parts_ref), custom_call_target="tpu_custom_call" | custom-call | tf_op jit(solution)/shard_map/normed/pallas_call | solution.py:94
  (1 shorter events, 0.0 us)
Async XLA Ops:
  6.2 11.6 %copy-start = (f32[128,2]{0,1:T(2,128)S(1)}, f32[128,2]{0,1:T(2,128)}, u32[]{:S(2)}) copy-start(f32[128,2]{0,1:T(2,128)} %param.6) | copy-start | bytes 3076
  6.2 11.6 %copy-start.1 = (f32[128]{0:T(128)S(1)}, f32[128]{0:T(128)}, u32[]{:S(2)}) copy-start(f32[128]{0:T(128)} %param.7) | copy-start | bytes 1540
  6.2 128.4 %all-to-all-start = ((bf16[32,2,200,128]{3,2,1,0:T(8,128)(2,1)}), bf16[32,2,200,128]{3,2,1,0:T(8,128)(2,1)S(1)}, u32[]{:S(2)}, u32[]{:S(2)}) async-start(bf16[32,2,200,128]{3,2,1,0:T(8,128)(2,1)} %packed.1), calls=%async_computation | async-start | bytes 6553600 | tf_op jit(solution)/shard_map/all_to_all | solution.py:116

commit v3 on v2

--- a/solution.py
+++ b/solution.py
@@ -4,6 +4,7 @@
 from jax.experimental import pallas as pl
 from jax.experimental.pallas import tpu as pltpu
 from jax.sharding import PartitionSpec as P
+
 
 PACK_GROUP = 4
 NORM_ROWS = 40
@@ -108,16 +109,21 @@
     )(pltpu.with_memory_space_constraint(parts, pltpu.VMEM))
 
 
+def sent_to_all(x, axis):
+    count = lax.axis_size(axis)
+    return lax.all_to_all(jnp.broadcast_to(x[None], (count, *x.shape)), axis, 0, 0, tiled=True)
+
+
 def body(master_down, second_down, router_weight, router_gain):
     shards = lax.axis_size("shard")
     experts, rows, lanes = master_down.shape
     cut = (experts, shards, rows // shards, lanes)
+    part_router = (router_weight * router_gain[:, None]).astype(jnp.bfloat16)
+    row_router = sent_to_all(part_router, "shard").reshape(shards * lanes, -1).T
     sent = packed(master_down.reshape(cut), second_down.reshape(cut))
     received = lax.all_to_all(sent, "shard", 0, 0, tiled=True)
+    serve_router = lax.all_gather(row_router, "expert", axis=0, tiled=True).T
     final_down, scale_down = normed(received)
-    part_router = (router_weight * router_gain[:, None]).astype(jnp.bfloat16).T
-    row_router = lax.all_gather(part_router, "shard", axis=1, tiled=True)
-    serve_router = lax.all_gather(row_router, "expert", axis=0, tiled=True).T
     return (final_down, scale_down, serve_router)
 
 

time: 140 us -> 106 us (0.76); the launches traced: 137 us -> 105 us
  blocking collectives: 116 us -> 13.3 us
  waiting for transfers between devices: 0.01 us -> 62.3 us
  starting transfers between devices: 11.6 us -> 19 us
    all_gather x1 -> x0, blocking collectives: 103 us -> none  [body(): row_router = lax.all_gather(part_router, 'shard', axis=1, tiled=True)]
    all_to_all x1, waiting for transfers between devices: 0.01 us -> 59.9 us  [body(): received = lax.all_to_all(sent, 'shard', 0, 0, tiled=True)]
    all_to_all x0 -> x1, starting transfers between devices: none -> 11.6 us  [sent_to_all(): lax.all_to_all(jnp.broadcast_to(x[None], (count, *x.shape)), axis, 0, 0,...]
    all_to_all x1, starting transfers between devices: 11.6 us -> 7.44 us  [body(): received = lax.all_to_all(sent, 'shard', 0, 0, tiled=True)]
    all_to_all x0 -> x1, waiting for transfers between devices: none -> 2.35 us  [sent_to_all(): lax.all_to_all(jnp.broadcast_to(x[None], (count, *x.shape)), axis, 0, 0,...]
  transfers between devices with their start and end apart: 1 -> 2, of which waited for: 0 -> 2; matrix products, arithmetic and copies ran while one was open for 1% -> 1% of each run, Pallas kernels for 0% -> 5%
where the time goes in v3:
time: 106 us; the launch traced here: 105 us
  waiting for transfers between devices  62.3 us (59%)
  starting transfers between devices  19 us (18%)
  blocking collectives  13.3 us (13%)
  Pallas kernels  8.25 us (8%)
  local copies, waits for them, and re-layouts  1.32 us (1%)
    all_to_all x1, waiting for transfers between devices, body(): received = lax.all_to_all(sent, 'shard', 0, 0, tiled=True)  59.9 us
    all_gather x1, blocking collectives, body(): serve_router = lax.all_gather(row_router, 'expert', axis=0, tiled=True).T  13.3 us
    all_to_all x1, starting transfers between devices, sent_to_all(): lax.all_to_all(jnp.broadcast_to(x[None], (count, *x.shape)), axis, 0, 0,...  11.6 us
    all_to_all x1, starting transfers between devices, body(): received = lax.all_to_all(sent, 'shard', 0, 0, tiled=True)  7.44 us
    pallas_call x1, Pallas kernels, packed(): pl.pallas_call(packed_kernel, in_specs=[pl.BlockSpec(memory_space=pl.ANY)...  5.55 us
    pallas_call x1, Pallas kernels, normed(): pl.pallas_call(normed_kernel, in_specs=[pl.BlockSpec(memory_space=pltpu.V...  2.7 us
    all_to_all x1, waiting for transfers between devices, sent_to_all(): lax.all_to_all(jnp.broadcast_to(x[None], (count, *x.shape)), axis, 0, 0,...  2.35 us
  transfers between devices with their start and end apart: 2, of which 2 were waited for; matrix products, arithmetic and copies ran while one was open for 1% of the time, Pallas kernels for 5%

profile of v3, /device:TPU:6, one launch (start us, length us, event | category | flops | bytes accessed | tf_op | source)
XLA Modules:
  0.0 105.5 jit_solution(6934754761389565263)
XLA Ops:
  0.6 0.7 multiply_convert_fusion
  1.3 0.6 broadcast_in_dim.2
  1.9 11.6 %all-to-all-start.1 = ((bf16[32,128,2]{1,2,0:T(2,128)(2,1)}), bf16[32,128,2]{1,2,0:T(2,128)(2,1)S(1)}, u32[]{:S(2)}, u32[]{:S(2)}) async-start(bf16[32,128,2]{1,2,0:T(2,128)(2,1)} %broadcast_in_dim.2), calls=%async_computation.1 | async-start | bytes 32768 | tf_op jit(solution)/shard_map/all_to_all | solution.py:114
  13.5 5.6 %packed.1 = bf16[32,2,200,128]{3,2,1,0:T(8,128)(2,1)} custom-call(f32[2,32,200,128]{3,2,1,0:T(8,128)} %bitcast.8, bf16[2,32,200,128]{3,2,1,0:T(8,128)(2,1)} %bitcast.9), custom_call_target="tpu_custom_call" | custom-call | tf_op jit(solution)/shard_map/packed/pallas_call | solution.py:45
  19.1 2.4 %all-to-all-done.1 = bf16[32,128,2]{1,2,0:T(2,128)(2,1)S(1)} async-done(((bf16[32,128,2]{1,2,0:T(2,128)(2,1)}), bf16[32,128,2]{1,2,0:T(2,128)(2,1)S(1)}, u32[]{:S(2)}, u32[]{:S(2)}) %all-to-all-start.1) | async-done | bytes 16416 | tf_op jit(solution)/shard_map/all_to_all | solution.py:114
  21.4 7.4 %all-to-all-start = ((bf16[32,2,200,128]{3,2,1,0:T(8,128)(2,1)}), bf16[32,2,200,128]{3,2,1,0:T(8,128)(2,1)S(1)}, u32[]{:S(2)}, u32[]{:S(2)}) async-start(bf16[32,2,200,128]{3,2,1,0:T(8,128)(2,1)} %packed.1), calls=%async_computation | async-start | bytes 6553600 | tf_op jit(solution)/shard_map/all_to_all | solution.py:124
  28.9 13.3 %all-gather = bf16[8,2,4096]{2,1,0:T(2,128)(2,1)S(1)} all-gather(bf16[1,2,4096]{2,1,0:T(2,128)(2,1)S(1)} %bitcast.11), channel_id=1, replica_groups=mesh['expert'=8,'shard'=32] {'expert'}, dimensions={0}, use_global_device_ids=true | all-gather | bytes 147456 | tf_op jit(solution)/shard_map/all_gather | solution.py:125
  42.1 0.7 reshape.21
  42.8 59.9 %all-to-all-done.parts_ref = bf16[32,2,200,128]{3,2,1,0:T(8,128)(2,1)S(1)} async-done(((bf16[32,2,200,128]{3,2,1,0:T(8,128)(2,1)}), bf16[32,2,200,128]{3,2,1,0:T(8,128)(2,1)S(1)}, u32[]{:S(2)}, u32[]{:S(2)}) %all-to-all-start) | async-done | bytes 3276832 | tf_op jit(solution)/shard_map/all_to_all | solution.py:124
  102.8 2.7 %normed.1 = (bf16[2,200,4096]{2,1,0:T(8,128)(2,1)}, f32[2,200]{1,0:T(2,128)}) custom-call(bf16[32,2,200,128]{3,2,1,0:T(8,128)(2,1)S(1)} %all-to-all-done.parts_ref), custom_call_target="tpu_custom_call" | custom-call | tf_op jit(solution)/shard_map/normed/pallas_call | solution.py:95
Async XLA Ops:
  1.9 19.5 %all-to-all-start.1 = ((bf16[32,128,2]{1,2,0:T(2,128)(2,1)}), bf16[32,128,2]{1,2,0:T(2,128)(2,1)S(1)}, u32[]{:S(2)}, u32[]{:S(2)}) async-start(bf16[32,128,2]{1,2,0:T(2,128)(2,1)} %broadcast_in_dim.2), calls=%async_computation.1 | async-start | bytes 32768 | tf_op jit(solution)/shard_map/all_to_all | solution.py:114
  21.4 81.4 %all-to-all-start = ((bf16[32,2,200,128]{3,2,1,0:T(8,128)(2,1)}), bf16[32,2,200,128]{3,2,1,0:T(8,128)(2,1)S(1)}, u32[]{:S(2)}, u32[]{:S(2)}) async-start(bf16[32,2,200,128]{3,2,1,0:T(8,128)(2,1)} %packed.1), calls=%async_computation | async-start | bytes 6553600 | tf_op jit(solution)/shard_map/all_to_all | solution.py:124

commit v4 on v2

--- a/solution.py
+++ b/solution.py
@@ -5,8 +5,10 @@
 from jax.experimental.pallas import tpu as pltpu
 from jax.sharding import PartitionSpec as P
 
+
 PACK_GROUP = 4
 NORM_ROWS = 40
+RING, CROSS = 8, 4
 
 
 def packed_kernel(master_ref, second_ref, out_ref, master_vmem, second_vmem, out_vmem, master_sem, second_sem, out_sem):
@@ -58,7 +60,9 @@
     )(master, second)
 
 
-def normed_kernel(parts_ref, out_ref, scale_ref, out_vmem, total_vmem, sems):
+def normed_kernel(places, parts_ref, *refs):
+    columns = refs[:-6]
+    out_ref, scale_ref, router_ref, out_vmem, total_vmem, sems = refs[-6:]
     shards, experts, rows, lanes = parts_ref.shape
     blocks = rows // NORM_ROWS
 
@@ -80,6 +84,10 @@
                 part = parts_ref[s, expert, at].astype(jnp.float32)
                 out_vmem[expert, at, pl.ds(s * lanes, lanes)] = (part * inverse).astype(jnp.bfloat16)
             copy(expert, block).start()
+    for i, column in enumerate(columns):
+        for j in range(column.shape[0]):
+            at = pl.multiple_of(places[i * column.shape[0] + j] * lanes, lanes)
+            router_ref[:, pl.ds(at, lanes)] = column[j]
     for expert in range(experts):
         turned = jnp.transpose(total_vmem[expert])
         scale_ref[pl.ds(expert, 1)] = jnp.sqrt(jnp.sum(turned, axis=0, keepdims=True))
@@ -88,16 +96,17 @@
             copy(expert, block).wait()
 
 
-def normed(parts):
+def normed(parts, places, columns):
     shards, experts, rows, lanes = parts.shape
     width = shards * lanes
     return pl.pallas_call(
         normed_kernel,
-        in_specs=[pl.BlockSpec(memory_space=pltpu.VMEM)],
-        out_specs=[pl.BlockSpec(memory_space=pl.ANY), pl.BlockSpec(memory_space=pltpu.VMEM)],
+        in_specs=[pl.BlockSpec(memory_space=pltpu.SMEM)] + [pl.BlockSpec(memory_space=pltpu.VMEM)] * (1 + len(columns)),
+        out_specs=[pl.BlockSpec(memory_space=pl.ANY)] + [pl.BlockSpec(memory_space=pltpu.VMEM)] * 2,
         out_shape=[
             jax.ShapeDtypeStruct((experts, rows, width), jnp.bfloat16),
             jax.ShapeDtypeStruct((experts, rows), jnp.float32),
+            jax.ShapeDtypeStruct((columns[0].shape[1], width), jnp.bfloat16),
         ],
         scratch_shapes=[
             pltpu.VMEM((experts, rows, width), jnp.bfloat16),
@@ -105,20 +114,39 @@
             pltpu.SemaphoreType.DMA((experts * rows // NORM_ROWS,)),
         ],
         name="normed",
-    )(pltpu.with_memory_space_constraint(parts, pltpu.VMEM))
+    )(places, *[pltpu.with_memory_space_constraint(x, pltpu.VMEM) for x in (parts, *columns)])
+
+
+def moved(x, dz, dx):
+    pairs = [
+        (z * CROSS + c, ((z + dz) % RING) * CROSS + (c + dx) % CROSS) for z in range(RING) for c in range(CROSS)
+    ]
+    return lax.ppermute(x, "shard", pairs)
 
 
 def body(master_down, second_down, router_weight, router_gain):
     shards = lax.axis_size("shard")
     experts, rows, lanes = master_down.shape
     cut = (experts, shards, rows // shards, lanes)
+    me = lax.axis_index("shard")
+    z, c = me >> 2, me & (CROSS - 1)
+    dz = jnp.array([s // CROSS for s in range(shards)], jnp.int32)
+    dx = jnp.array([s % CROSS for s in range(shards)], jnp.int32)
+    places = (((z - dz) & (RING - 1)) << 2) | ((c - dx) & (CROSS - 1))
     sent = packed(master_down.reshape(cut), second_down.reshape(cut))
     received = lax.all_to_all(sent, "shard", 0, 0, tiled=True)
-    final_down, scale_down = normed(received)
     part_router = (router_weight * router_gain[:, None]).astype(jnp.bfloat16).T
-    row_router = lax.all_gather(part_router, "shard", axis=1, tiled=True)
-    serve_router = lax.all_gather(row_router, "expert", axis=0, tiled=True).T
-    return (final_down, scale_down, serve_router)
+    column = lax.all_gather(part_router, "expert", axis=0, tiled=True)
+    pieces = [column]
+    for step in range(1, CROSS):
+        pieces.append(moved(column, 0, step))
+    stacked = jnp.stack(pieces)
+    columns = [stacked]
+    for step in (4, 3, 5, 2, 6, 1, 7):
+        columns.append(moved(stacked, step, 0))
+    columns = [columns[0]] + [columns[1 + (4, 3, 5, 2, 6, 1, 7).index(step)] for step in range(1, RING)]
+    final_down, scale_down, serve_router = normed(received, places, columns)
+    return (final_down, scale_down, serve_router.T)
 
 
 def solution(mesh):

time: 140 us -> 102 us (0.73); the launches traced: 137 us -> 101 us
  blocking collectives: 116 us -> 10.8 us
  waiting for transfers between devices: 0.01 us -> 50.4 us
  starting transfers between devices: 11.6 us -> 29.9 us
    all_gather x2 -> x1, blocking collectives: 116 us -> 10.8 us  [body(): column = lax.all_gather(part_router, 'expert', axis=0, tiled=True)]
    ppermute x0 -> x10, waiting for transfers between devices: none -> 50.4 us  [moved(): return lax.ppermute(x, 'shard', pairs)]
    ppermute x0 -> x10, starting transfers between devices: none -> 18.2 us  [moved(): return lax.ppermute(x, 'shard', pairs)]
  transfers between devices with their start and end apart: 1 -> 11, of which waited for: 0 -> 4; matrix products, arithmetic and copies ran while one was open for 1% -> 1% of each run, Pallas kernels for 0% -> 0%
where the time goes in v4:
time: 102 us; the launch traced here: 101 us
  waiting for transfers between devices  50.4 us (49%)
  starting transfers between devices  29.9 us (29%)
  blocking collectives  10.8 us (11%)
  Pallas kernels  9 us (9%)
    ppermute x10, waiting for transfers between devices, moved(): return lax.ppermute(x, 'shard', pairs)  50.4 us
    ppermute x10, starting transfers between devices, moved(): return lax.ppermute(x, 'shard', pairs)  18.2 us
    all_to_all x1, starting transfers between devices, body(): received = lax.all_to_all(sent, 'shard', 0, 0, tiled=True)  11.7 us
    all_gather x1, blocking collectives, body(): column = lax.all_gather(part_router, 'expert', axis=0, tiled=True)  10.8 us
    pallas_call x1, Pallas kernels, packed(): pl.pallas_call(packed_kernel, in_specs=[pl.BlockSpec(memory_space=pl.ANY)...  5.55 us
    pallas_call x1, Pallas kernels, normed(): pl.pallas_call(normed_kernel, in_specs=[pl.BlockSpec(memory_space=pltpu.S...  3.45 us
  transfers between devices with their start and end apart: 11, of which 4 were waited for; matrix products, arithmetic and copies ran while one was open for 1% of the time, Pallas kernels for 0%

profile of v4, /device:TPU:6, one launch (start us, length us, event | category | flops | bytes accessed | tf_op | source)
XLA Modules:
  0.0 101.4 jit_solution(15943659726318232552)
XLA Ops:
  0.6 5.5 %packed.1 = bf16[32,2,200,128]{3,2,1,0:T(8,128)(2,1)} custom-call(f32[2,32,200,128]{3,2,1,0:T(8,128)} %bitcast.12, bf16[2,32,200,128]{3,2,1,0:T(8,128)(2,1)} %bitcast.13), custom_call_target="tpu_custom_call" | custom-call | tf_op jit(solution)/shard_map/packed/pallas_call | solution.py:46
  6.2 0.0 copy-start
  6.2 0.0 copy-start.3
  6.2 0.0 copy-start.1
  6.2 0.0 copy-start.2
  6.2 11.7 %all-to-all-start = ((bf16[32,2,200,128]{3,2,1,0:T(8,128)(2,1)}), bf16[32,2,200,128]{3,2,1,0:T(8,128)(2,1)S(1)}, u32[]{:S(2)}, u32[]{:S(2)}) async-start(bf16[32,2,200,128]{3,2,1,0:T(8,128)(2,1)} %packed.1), calls=%async_computation | async-start | bytes 6553600 | tf_op jit(solution)/shard_map/all_to_all | solution.py:137
  17.9 0.0 copy-done
  18.0 0.0 copy-done.3
  18.0 10.8 %all-gather = bf16[8,2,128]{2,1,0:T(2,128)(2,1)S(1)} all-gather(bf16[1,2,128]{2,1,0:T(2,128)(2,1)S(1)} %fusion), channel_id=1, replica_groups=mesh['expert'=8,'shard'=32] {'expert'}, dimensions={0}, use_global_device_ids=true | all-gather | bytes 4608 | tf_op jit(solution)/shard_map/all_gather | solution.py:139
  28.8 1.5 %collective-permute-start.1 = (bf16[16,128]{1,0:T(8,128)(2,1)S(1)}, bf16[16,128]{1,0:T(8,128)(2,1)S(1)}, u32[]{:S(2)}, u32[]{:S(2)}) collective-permute-start(bf16[16,128]{1,0:T(8,128)(2,1)S(1)} %bitcast.14), channel_id=1, source_target_pairs={{0,2},{1,3},{2,0},{3,1},{4,6},{5,7},{6,4},{7,5},{8,10},{9,11},{10,... | collective-permute-start | bytes 12296 | tf_op jit(solution)/shard_map/ppermute | solution.py:124
  30.2 2.1 %collective-permute-start = (bf16[16,128]{1,0:T(8,128)(2,1)S(1)}, bf16[16,128]{1,0:T(8,128)(2,1)S(1)}, u32[]{:S(2)}, u32[]{:S(2)}) collective-permute-start(bf16[16,128]{1,0:T(8,128)(2,1)S(1)} %bitcast.15), channel_id=1, source_target_pairs={{0,1},{1,2},{2,3},{3,0},{4,5},{5,6},{6,7},{7,4},{8,9},{9,10},{10,1... | collective-permute-start | bytes 12296 | tf_op jit(solution)/shard_map/ppermute | solution.py:124
  32.3 0.0 collective-permute-start.2
  32.3 1.8 %collective-permute-done.1 = bf16[16,128]{1,0:T(8,128)(2,1)S(1)} collective-permute-done((bf16[16,128]{1,0:T(8,128)(2,1)S(1)}, bf16[16,128]{1,0:T(8,128)(2,1)S(1)}, u32[]{:S(2)}, u32[]{:S(2)}) %collective-permute-start.1) | collective-permute-done | bytes 4128 | tf_op jit(solution)/shard_map/ppermute | solution.py:124
  34.1 0.0 collective-permute-done
  34.1 3.1 %collective-permute-done.2 = bf16[16,128]{1,0:T(8,128)(2,1)S(1)} collective-permute-done((bf16[16,128]{1,0:T(8,128)(2,1)S(1)}, bf16[16,128]{1,0:T(8,128)(2,1)S(1)}, u32[]{:S(2)}, u32[]{:S(2)}) %collective-permute-start.2) | collective-permute-done | bytes 4128 | tf_op jit(solution)/shard_map/ppermute | solution.py:124
  37.2 4.6 %collective-permute-start.9 = (bf16[4,16,128]{2,1,0:T(8,128)(2,1)S(1)}, bf16[4,16,128]{2,1,0:T(8,128)(2,1)S(1)}, u32[]{:S(2)}, u32[]{:S(2)}) collective-permute-start(bf16[4,16,128]{2,1,0:T(8,128)(2,1)S(1)} %pad_maximum_fusion.refs_0_), channel_id=1, source_target_pairs={{0,28},{1,29},{2,30},{3,31},{4,0},{5,1},{6,2},{7,3},{8,4},{9,5},{1... | collective-permute-start | bytes 49160 | tf_op jit(solution)/shard_map/ppermute | solution.py:124
  41.8 0.4 collective-permute-start.8
  42.2 1.5 %collective-permute-start.7 = (bf16[4,16,128]{2,1,0:T(8,128)(2,1)S(1)}, bf16[4,16,128]{2,1,0:T(8,128)(2,1)S(1)}, u32[]{:S(2)}, u32[]{:S(2)}) collective-permute-start(bf16[4,16,128]{2,1,0:T(8,128)(2,1)S(1)} %pad_maximum_fusion.refs_0_), channel_id=1, source_target_pairs={{0,20},{1,21},{2,22},{3,23},{4,24},{5,25},{6,26},{7,27},{8,28},{9,... | collective-permute-start | bytes 49160 | tf_op jit(solution)/shard_map/ppermute | solution.py:124
  43.7 4.1 %collective-permute-start.6 = (bf16[4,16,128]{2,1,0:T(8,128)(2,1)S(1)}, bf16[4,16,128]{2,1,0:T(8,128)(2,1)S(1)}, u32[]{:S(2)}, u32[]{:S(2)}) collective-permute-start(bf16[4,16,128]{2,1,0:T(8,128)(2,1)S(1)} %pad_maximum_fusion.refs_0_), channel_id=1, source_target_pairs={{0,16},{1,17},{2,18},{3,19},{4,20},{5,21},{6,22},{7,23},{8,24},{9,... | collective-permute-start | bytes 49160 | tf_op jit(solution)/shard_map/ppermute | solution.py:124
  47.8 0.0 collective-permute-start.5
  47.8 44.3 %collective-permute-done.9.refs_7_ = bf16[4,16,128]{2,1,0:T(8,128)(2,1)S(1)} collective-permute-done((bf16[4,16,128]{2,1,0:T(8,128)(2,1)S(1)}, bf16[4,16,128]{2,1,0:T(8,128)(2,1)S(1)}, u32[]{:S(2)}, u32[]{:S(2)}) %collective-permute-start.9) | collective-permute-done | bytes 16416 | tf_op jit(solution)/shard_map/ppermute | solution.py:124
  92.1 0.0 collective-permute-start.4
  92.1 0.0 collective-permute-done.8.refs_6_
  92.1 4.1 %collective-permute-start.3 = (bf16[4,16,128]{2,1,0:T(8,128)(2,1)S(1)}, bf16[4,16,128]{2,1,0:T(8,128)(2,1)S(1)}, u32[]{:S(2)}, u32[]{:S(2)}) collective-permute-start(bf16[4,16,128]{2,1,0:T(8,128)(2,1)S(1)} %pad_maximum_fusion.refs_0_), channel_id=1, source_target_pairs={{0,4},{1,5},{2,6},{3,7},{4,8},{5,9},{6,10},{7,11},{8,12},{9,13},{1... | collective-permute-start | bytes 49160 | tf_op jit(solution)/shard_map/ppermute | solution.py:124
  96.2 0.0 copy-done.1
  96.2 0.0 copy-done.2
  96.2 0.5 fusion.1.places
  96.8 0.0 collective-permute-done.7.refs_5_
  96.8 0.0 collective-permute-done.6.refs_4_
  96.8 0.0 collective-permute-done.5.refs_3_
  96.8 1.2 %collective-permute-done.4.refs_2_ = bf16[4,16,128]{2,1,0:T(8,128)(2,1)S(1)} collective-permute-done((bf16[4,16,128]{2,1,0:T(8,128)(2,1)S(1)}, bf16[4,16,128]{2,1,0:T(8,128)(2,1)S(1)}, u32[]{:S(2)}, u32[]{:S(2)}) %collective-permute-start.4) | collective-permute-done | bytes 16416 | tf_op jit(solution)/shard_map/ppermute | solution.py:124
  98.0 0.0 collective-permute-done.3.refs_1_
  98.0 0.0 all-to-all-done.parts_ref
  98.0 3.4 %normed.1 = (bf16[2,200,4096]{2,1,0:T(8,128)(2,1)}, f32[2,200]{1,0:T(2,128)}, bf16[16,4096]{1,0:T(8,128)(2,1)}) custom-call(s32[32]{0:T(128)} %fusion.1.places, bf16[32,2,200,128]{3,2,1,0:T(8,128)(2,1)S(1)} %all-to-all-done.parts_ref, bf16[4,16,128]{2,1,0:T(8,128)(2,1)S(1)} %pad_maximum_fusion.refs_0_, ...), custom_call_target="tpu_custom_call" | custom-call | tf_op jit(solution)/shard_map/normed/pallas_call | solution.py:102
  (2 shorter events, 0.0 us)
Async XLA Ops:
  6.2 11.8 %copy-start = (f32[128,2]{0,1:T(2,128)S(1)}, f32[128,2]{0,1:T(2,128)}, u32[]{:S(2)}) copy-start(f32[128,2]{0,1:T(2,128)} %param.8) | copy-start | bytes 3076
  6.2 11.8 %copy-start.3 = (f32[128]{0:T(128)S(1)}, f32[128]{0:T(128)}, u32[]{:S(2)}) copy-start(f32[128]{0:T(128)} %param.9) | copy-start | bytes 1540
  6.2 90.0 %copy-start.1 = (s32[32]{0:T(128)S(1)}, s32[32]{0:T(128)}, u32[]{:S(2)}) copy-start(s32[32]{0:T(128)} %constant.22) | copy-start | bytes 388
  6.2 90.0 %copy-start.2 = (s32[32]{0:T(128)S(1)}, s32[32]{0:T(128)}, u32[]{:S(2)}) copy-start(s32[32]{0:T(128)} %constant.21) | copy-start | bytes 388
  6.2 91.8 %all-to-all-start = ((bf16[32,2,200,128]{3,2,1,0:T(8,128)(2,1)}), bf16[32,2,200,128]{3,2,1,0:T(8,128)(2,1)S(1)}, u32[]{:S(2)}, u32[]{:S(2)}) async-start(bf16[32,2,200,128]{3,2,1,0:T(8,128)(2,1)} %packed.1), calls=%async_computation | async-start | bytes 6553600 | tf_op jit(solution)/shard_map/all_to_all | solution.py:137
  28.8 5.4 %collective-permute-start.1 = (bf16[16,128]{1,0:T(8,128)(2,1)S(1)}, bf16[16,128]{1,0:T(8,128)(2,1)S(1)}, u32[]{:S(2)}, u32[]{:S(2)}) collective-permute-start(bf16[16,128]{1,0:T(8,128)(2,1)S(1)} %bitcast.14), channel_id=1, source_target_pairs={{0,2},{1,3},{2,0},{3,1},{4,6},{5,7},{6,4},{7,5},{8,10},{9,11},{10,... | collective-permute-start | bytes 12296 | tf_op jit(solution)/shard_map/ppermute | solution.py:124
  30.2 3.9 %collective-permute-start = (bf16[16,128]{1,0:T(8,128)(2,1)S(1)}, bf16[16,128]{1,0:T(8,128)(2,1)S(1)}, u32[]{:S(2)}, u32[]{:S(2)}) collective-permute-start(bf16[16,128]{1,0:T(8,128)(2,1)S(1)} %bitcast.15), channel_id=1, source_target_pairs={{0,1},{1,2},{2,3},{3,0},{4,5},{5,6},{6,7},{7,4},{8,9},{9,10},{10,1... | collective-permute-start | bytes 12296 | tf_op jit(solution)/shard_map/ppermute | solution.py:124
  32.3 4.9 %collective-permute-start.2 = (bf16[16,128]{1,0:T(8,128)(2,1)S(1)}, bf16[16,128]{1,0:T(8,128)(2,1)S(1)}, u32[]{:S(2)}, u32[]{:S(2)}) collective-permute-start(bf16[16,128]{1,0:T(8,128)(2,1)S(1)} %bitcast.16), channel_id=1, source_target_pairs={{0,3},{1,0},{2,1},{3,2},{4,7},{5,4},{6,5},{7,6},{8,11},{9,8},{10,9... | collective-permute-start | bytes 12296 | tf_op jit(solution)/shard_map/ppermute | solution.py:124
  37.2 54.9 %collective-permute-start.9 = (bf16[4,16,128]{2,1,0:T(8,128)(2,1)S(1)}, bf16[4,16,128]{2,1,0:T(8,128)(2,1)S(1)}, u32[]{:S(2)}, u32[]{:S(2)}) collective-permute-start(bf16[4,16,128]{2,1,0:T(8,128)(2,1)S(1)} %pad_maximum_fusion.refs_0_), channel_id=1, source_target_pairs={{0,28},{1,29},{2,30},{3,31},{4,0},{5,1},{6,2},{7,3},{8,4},{9,5},{1... | collective-permute-start | bytes 49160 | tf_op jit(solution)/shard_map/ppermute | solution.py:124
  41.8 50.3 %collective-permute-start.8 = (bf16[4,16,128]{2,1,0:T(8,128)(2,1)S(1)}, bf16[4,16,128]{2,1,0:T(8,128)(2,1)S(1)}, u32[]{:S(2)}, u32[]{:S(2)}) collective-permute-start(bf16[4,16,128]{2,1,0:T(8,128)(2,1)S(1)} %pad_maximum_fusion.refs_0_), channel_id=1, source_target_pairs={{0,24},{1,25},{2,26},{3,27},{4,28},{5,29},{6,30},{7,31},{8,0},{9,1... | collective-permute-start | bytes 49160 | tf_op jit(solution)/shard_map/ppermute | solution.py:124
  42.2 54.5 %collective-permute-start.7 = (bf16[4,16,128]{2,1,0:T(8,128)(2,1)S(1)}, bf16[4,16,128]{2,1,0:T(8,128)(2,1)S(1)}, u32[]{:S(2)}, u32[]{:S(2)}) collective-permute-start(bf16[4,16,128]{2,1,0:T(8,128)(2,1)S(1)} %pad_maximum_fusion.refs_0_), channel_id=1, source_target_pairs={{0,20},{1,21},{2,22},{3,23},{4,24},{5,25},{6,26},{7,27},{8,28},{9,... | collective-permute-start | bytes 49160 | tf_op jit(solution)/shard_map/ppermute | solution.py:124
  43.7 53.1 %collective-permute-start.6 = (bf16[4,16,128]{2,1,0:T(8,128)(2,1)S(1)}, bf16[4,16,128]{2,1,0:T(8,128)(2,1)S(1)}, u32[]{:S(2)}, u32[]{:S(2)}) collective-permute-start(bf16[4,16,128]{2,1,0:T(8,128)(2,1)S(1)} %pad_maximum_fusion.refs_0_), channel_id=1, source_target_pairs={{0,16},{1,17},{2,18},{3,19},{4,20},{5,21},{6,22},{7,23},{8,24},{9,... | collective-permute-start | bytes 49160 | tf_op jit(solution)/shard_map/ppermute | solution.py:124
  47.8 49.0 %collective-permute-start.5 = (bf16[4,16,128]{2,1,0:T(8,128)(2,1)S(1)}, bf16[4,16,128]{2,1,0:T(8,128)(2,1)S(1)}, u32[]{:S(2)}, u32[]{:S(2)}) collective-permute-start(bf16[4,16,128]{2,1,0:T(8,128)(2,1)S(1)} %pad_maximum_fusion.refs_0_), channel_id=1, source_target_pairs={{0,12},{1,13},{2,14},{3,15},{4,16},{5,17},{6,18},{7,19},{8,20},{9,... | collective-permute-start | bytes 49160 | tf_op jit(solution)/shard_map/ppermute | solution.py:124
  92.1 5.8 %collective-permute-start.4 = (bf16[4,16,128]{2,1,0:T(8,128)(2,1)S(1)}, bf16[4,16,128]{2,1,0:T(8,128)(2,1)S(1)}, u32[]{:S(2)}, u32[]{:S(2)}) collective-permute-start(bf16[4,16,128]{2,1,0:T(8,128)(2,1)S(1)} %pad_maximum_fusion.refs_0_), channel_id=1, source_target_pairs={{0,8},{1,9},{2,10},{3,11},{4,12},{5,13},{6,14},{7,15},{8,16},{9,17... | collective-permute-start | bytes 49160 | tf_op jit(solution)/shard_map/ppermute | solution.py:124
  92.1 5.8 %collective-permute-start.3 = (bf16[4,16,128]{2,1,0:T(8,128)(2,1)S(1)}, bf16[4,16,128]{2,1,0:T(8,128)(2,1)S(1)}, u32[]{:S(2)}, u32[]{:S(2)}) collective-permute-start(bf16[4,16,128]{2,1,0:T(8,128)(2,1)S(1)} %pad_maximum_fusion.refs_0_), channel_id=1, source_target_pairs={{0,4},{1,5},{2,6},{3,7},{4,8},{5,9},{6,10},{7,11},{8,12},{9,13},{1... | collective-permute-start | bytes 49160 | tf_op jit(solution)/shard_map/ppermute | solution.py:124
